TPU v7x, 512 devices: a whole 4x8x8 slice. The times are simulated.
512 devices in a mesh: row: 32 (over z_lo, y, core), col: 16 (over z_hi, x).
Axes of the slice: x: 4, y: 8, z: 8 (z_hi: 4, z_lo: 2; z = z_hi * 2 + z_lo), core: 2. Of those that a mesh axis runs over, the one named last changes fastest.
Arguments:
- pixels: float32 [8, 3, 1024, 2048], P(None, None, 'row', 'col'), may hold values from -6 to 6
- factor: float32 [1024, 512], P('row'), may hold values from -6 to 6
Outputs:
- gram: float32 [1024, 1024], P('row', 'col')
- projected: float32 [1024, 512], P('col', 'row')
All inputs are finite; a program needn't handle non-finite values.
Results may differ from a plain program's by a relative error of at most 0.000075.
Values sent between devices are 32-bit elements; how exact they have to be, the bound alone decides.
No kernel may reach another device: no remote copies, remote signals or barrier semaphores. Data moves between devices by JAX's collectives and lax.ppermute only.
A program may use at most 64 MiB of HBM per device.

v0:
```python
import jax
import jax.numpy as jnp
from jax import lax
from jax.sharding import PartitionSpec as P


def split_up(array, dim, size):
    before, after = (array.shape[:dim], array.shape[dim + 1 :])
    return jnp.moveaxis(array.reshape(*before, size, -1, *after), dim, 0)


def sum_at_owner(array, axis, dim):
    size = lax.axis_size(axis)
    parts = lax.all_to_all(split_up(array, dim, size), axis, 0, 0, tiled=True)
    return jnp.sum(parts, axis=0)


def pair_rows(own, others):
    return jnp.einsum(
        "vciw,vcjw->ij",
        own,
        others,
        precision=lax.Precision.HIGHEST,
        preferred_element_type=jnp.float32,
    )


def shards(pixels, factor):
    col_count = lax.axis_size("col")
    weight_scale = 1.0 / (pixels.shape[0] * pixels.shape[1] * pixels.shape[3] * col_count)
    partial_value = pair_rows(pixels, lax.all_gather(pixels, "row", axis=2, tiled=True))
    partial_value = partial_value * weight_scale
    block = sum_at_owner(partial_value, "col", 1)
    term = lax.dot_general(
        block,
        factor,
        (((0,), (0,)), ((), ())),
        precision=lax.Precision.HIGHEST,
        preferred_element_type=jnp.float32,
    )
    projected = sum_at_owner(term, "row", 1)
    return (block, projected)


def solution(mesh):
    in_specs = (P(None, None, "row", "col"), P("row", None))
    out_specs = (P("row", "col"), P("col", "row"))
    return jax.shard_map(shards, mesh=mesh, in_specs=in_specs, out_specs=out_specs, check_vma=False)
```

profile of v0, /device:TPU:1, one launch (start us, length us, event | category | flops | bytes accessed | tf_op | source)
XLA Modules:
  0.0 160.4 jit_solution(10644495970476327923)
XLA Ops:
  7.2 0.0 copy-start
  7.2 0.0 all-gather.2.cloned.1.call-start
  7.2 1.8 %copy.12 = f32[8,3,32,128]{3,2,0,1:T(8,128)} copy(f32[8,3,32,128]{3,2,1,0:T(8,128)} %param.2) | data formatting | bytes 786432 | tf_op args[0]
  9.0 0.0 all-gather.2.cloned.1.call-update
  9.0 89.4 %all-gather.2.cloned.1.call-done = f32[8,3,1024,128]{3,2,0,1:T(8,128)} async-done(((f32[8,3,32,128]{3,2,0,1:T(8,128)}), f32[8,3,1024,128]{3,2,0,1:T(8,128)}) %all-gather.2.cloned.1.call-update) | async-done | bytes 12582928 | tf_op jit(solution)/shard_map/all_gather | solution.py:31
  98.4 14.3 %fusion = f32[32,1024]{1,0:T(8,128)S(1)} fusion(f32[8,3,1024,128]{3,2,0,1:T(8,128)} %all-gather.2.cloned.1.call-done, f32[8,3,32,128]{3,2,1,0:T(8,128)} %param.2), kind=kOutput, calls=%fused_computation.2 | convolution fusion | flops 1207992320 | bytes 13107200 | tf_op jit(solution)/shard_map/vciw,vcjw->ij/dot_general | solution.py:19
  112.7 0.1 reshape.9
  112.8 0.1 copy.24
  112.9 0.8 reshape.12
  113.8 9.5 %all-to-all-start = ((f32[16,1,2048]{2,1,0:T(1,128)}), f32[16,1,2048]{2,1,0:T(1,128)S(1)}, u32[]{:S(2)}, u32[]{:S(2)}) async-start(f32[16,1,2048]{2,1,0:T(1,128)} %reshape.12), calls=%async_computation | async-start | bytes 262144 | tf_op jit(solution)/shard_map/all_to_all | solution.py:14
  123.3 0.0 copy-done
  123.3 0.1 copy.14
  123.4 9.2 %all-to-all-done = f32[16,1,2048]{2,1,0:T(1,128)S(1)} async-done(((f32[16,1,2048]{2,1,0:T(1,128)}), f32[16,1,2048]{2,1,0:T(1,128)S(1)}, u32[]{:S(2)}, u32[]{:S(2)}) %all-to-all-start) | async-done | bytes 131104 | tf_op jit(solution)/shard_map/all_to_all | solution.py:14
  132.6 0.5 broadcast
  133.1 0.9 reduce
  134.1 0.1 reshape.13
  134.2 0.0 copy-start.1
  134.2 0.4 convolution_bitcast_fusion
  134.6 0.2 copy.25
  134.8 0.2 reshape.14
  135.0 16.9 %all_to_all.10 = f32[32,1,1024]{2,1,0:T(1,128)S(1)} all-to-all(f32[32,1,1024]{2,1,0:T(1,128)S(1)} %reshape.14), channel_id=1, replica_groups=mesh['row'=32,'col'=16] {'row'}, dimensions={0} | all-to-all | bytes 262144 | tf_op jit(solution)/shard_map/all_to_all | solution.py:14
  151.9 1.0 reduce.1
  152.8 0.1 reshape.15
  152.9 0.6 bitcast_reduce_fusion
  153.6 0.0 copy-done.1
  (1 shorter events, 0.0 us)
Async XLA Ops:
  7.2 116.1 %copy-start = (f32[32,512]{1,0:T(8,128)S(1)}, f32[32,512]{1,0:T(8,128)}, u32[]{:S(2)}) copy-start(f32[32,512]{1,0:T(8,128)} %param.3) | copy-start | bytes 196612
  7.2 91.2 %all-gather.2.cloned.1.call-start = ((), (), s32[]{:S(2)}) async-start(), calls=%async_computation.2 | async-start | bytes 12976128 | tf_op jit(solution)/shard_map/all_gather | solution.py:31
  113.8 18.8 %all-to-all-start = ((f32[16,1,2048]{2,1,0:T(1,128)}), f32[16,1,2048]{2,1,0:T(1,128)S(1)}, u32[]{:S(2)}, u32[]{:S(2)}) async-start(f32[16,1,2048]{2,1,0:T(1,128)} %reshape.12), calls=%async_computation | async-start | bytes 262144 | tf_op jit(solution)/shard_map/all_to_all | solution.py:14
  134.2 19.4 %copy-start.1 = (f32[32,64]{1,0:T(8,128)}, f32[32,64]{1,0:T(8,128)S(1)}, u32[]{:S(2)}) copy-start(f32[32,64]{1,0:T(8,128)S(1)} %reduce_sum.18) | copy-start | bytes 24580
Sparse Core Ops, SparseCore 0:
  10.1 88.2 all-gather.1
where the time goes:
time: 161 us; the launch traced here: 160 us
  waiting for transfers between devices  98.6 us (61%)
  blocking collectives  16.9 us (10%)
  matrix products  14.7 us (9%)
  between operations  14.1 us (9%)
  starting transfers between devices  9.53 us (6%)
  local copies, waits for them, and re-layouts  3.99 us (2%)
  other arithmetic  2.57 us (2%)
    all_gather x1, waiting for transfers between devices, shards(): lax.all_gather(pixels, 'row', axis=2, tiled=True)  89.4 us
    all_to_all x1, blocking collectives, sum_at_owner(): parts = lax.all_to_all(split_up(array, dim, size), axis, 0, 0, tiled=True)  16.9 us
    dot_general x1, matrix products, pair_rows(): jnp.einsum('vciw,vcjw->ij', own, others, precision=lax.Precision.HIGHEST,...  14.3 us
    all_to_all x1, starting transfers between devices, sum_at_owner(): parts = lax.all_to_all(split_up(array, dim, size), axis, 0, 0, tiled=True)  9.49 us
    all_to_all x1, waiting for transfers between devices, sum_at_owner(): parts = lax.all_to_all(split_up(array, dim, size), axis, 0, 0, tiled=True)  9.19 us
  transfers between devices with their start and end apart: 2, of which 2 were waited for; matrix products, arithmetic and copies ran while one was open for 0% of the time, Pallas kernels for 0%

commit v1 on v0

v1 whole, which is shorter than its diff:
```python
import jax
import jax.numpy as jnp
from jax import lax
from jax.experimental import pallas as pl
from jax.experimental.pallas import tpu as pltpu
from jax.sharding import Mesh
from jax.sharding import PartitionSpec as P

AXES = ("zl", "y", "k", "zh", "x")
SIZES = (2, 8, 2, 4, 4)
ROW = ("zl", "y", "k")
COL = ("zh", "x")
PLANES, OWN, LANES = 3, 32, 128
DEPTH = PLANES * LANES
COUNT = 8 * 3 * 2048
NT = (((1,), (1,)), ((), ()))


def call(body, out, scratch=(), operands=1, scalars=0):
    vmem = pl.BlockSpec(memory_space=pltpu.VMEM)
    smem = pl.BlockSpec(memory_space=pltpu.SMEM)
    many = isinstance(out, tuple)
    return pl.pallas_call(
        body,
        out_shape=out,
        in_specs=[smem] * scalars + [vmem] * operands,
        out_specs=tuple(vmem for _ in out) if many else vmem,
        scratch_shapes=list(scratch),
    )


def f32(*shape):
    return jax.ShapeDtypeStruct(shape, jnp.float32)


def pair_body(place, rows, out, high, low):
    for x in range(4):
        for zl in range(2):
            for zh_lo in range(2):
                for k in range(2):
                    at = x * 256 + zl * 128 + zh_lo * 64 + k * 32
                    for p in range(PLANES):
                        v = rows[k, zl * 8 + zh_lo * 4 + x, p * OWN : (p + 1) * OWN, :]
                        h = v.astype(jnp.bfloat16)
                        high[at : at + OWN, p * LANES : (p + 1) * LANES] = h
                        low[at : at + OWN, p * LANES : (p + 1) * LANES] = (v - h.astype(jnp.float32)).astype(jnp.bfloat16)
    own = place[0] * 128 + place[1] * 32

    def own_rows(ref):
        return jnp.concatenate([ref[pl.ds(pl.multiple_of(own + (y % 4) * 256 + (y // 4) * 64, 32), OWN), :] for y in range(8)], axis=0)

    own_high, own_low = own_rows(high), own_rows(low)
    for x in range(4):
        h, l = high[x * 256 : (x + 1) * 256, :], low[x * 256 : (x + 1) * 256, :]
        g = lax.dot_general(own_high, l, NT, preferred_element_type=jnp.float32)
        g += lax.dot_general(own_low, h, NT, preferred_element_type=jnp.float32)
        g += lax.dot_general(own_high, h, NT, preferred_element_type=jnp.float32)
        out[x, 0] = g[:, :LANES]
        out[x, 1] = g[:, LANES:]


def fold_body(parts, out):
    left = lax.broadcasted_iota(jnp.int32, (16, LANES), 1) < 64
    for zh in range(2):
        for y in range(8):
            v = parts[0, zh, y * OWN : (y + 1) * OWN, :]
            for x in range(1, 4):
                v += parts[x, zh, y * OWN : (y + 1) * OWN, :]
            a, b = v[:16], v[16:]
            out[zh * 2, y] = jnp.where(left, a, pltpu.roll(b, 64, 1))
            out[zh * 2 + 1, y] = jnp.where(left, pltpu.roll(a, 64, 1), b)


def term_body(parts, factor, gram, term):
    g = jnp.sum(parts[...], axis=0) / COUNT
    block = jnp.concatenate([g[:, :64], g[:, 64:]], axis=0)
    gram[...] = block
    t = lax.dot_general(
        factor[...], block, (((0,), (0,)), ((), ())), precision=lax.Precision.HIGHEST, preferred_element_type=jnp.float32
    )
    for r in range(32):
        term[r] = jnp.concatenate([t[r * 16 : r * 16 + 8], t[r * 16 + 8 : r * 16 + 16]], axis=1)


def close_body(parts, out):
    v = jnp.sum(parts[...], axis=0)
    out[...] = jnp.concatenate([v[:, :64], v[:, 64:]], axis=0)


def swap(array, axes):
    return lax.all_to_all(array, axes, 0, 0, tiled=True)


def shards(pixels, factor):
    place = jnp.stack([lax.axis_index("zl"), lax.axis_index("k")]).astype(jnp.int32)
    own = pixels.reshape(8, PLANES * OWN, LANES)
    rows = swap(jnp.broadcast_to(own[None], (2, *own.shape)).reshape(16, *own.shape[1:]), ("zl", "y"))
    rows = swap(jnp.broadcast_to(rows[None], (2, *rows.shape)), "k")
    wide = pltpu.VMEM((1024, DEPTH), jnp.bfloat16)
    partial_gram = call(pair_body, f32(4, 2, 256, LANES), (wide, wide), 1, 1)(place, rows)
    partial_gram = swap(partial_gram.reshape(4, 512, LANES), "x").reshape(4, 2, 256, LANES)
    folded = call(fold_body, f32(4, 8, 16, LANES))(partial_gram)
    folded = swap(folded.reshape(32, 16, LANES), ("zh", "y"))
    gram, term = call(term_body, (f32(32, 64), f32(32, 8, LANES)), (), 2)(folded, factor)
    projected = call(close_body, f32(16, 64))(swap(term, ROW))
    return gram, projected.T


def solution(mesh):
    split = Mesh(mesh.devices.reshape(SIZES), AXES)
    in_specs = (P(None, None, ROW, COL), P(ROW, None))
    out_specs = (P(ROW, COL), P(COL, ROW))
    return jax.shard_map(shards, mesh=split, in_specs=in_specs, out_specs=out_specs, check_vma=False)
```

time: 161 us -> 110 us (0.68)
  waiting for transfers between devices: 98.6 us -> 19.2 us
  blocking collectives: 16.9 us -> 67.5 us
  matrix products: 14.7 us -> 0 us
  between operations: 14.1 us -> 0.66 us
  Pallas kernels: 0 us -> 9.41 us
  other arithmetic: 2.57 us -> 0.65 us
  local copies, waits for them, and re-layouts: 3.99 us -> 2.17 us
    all_gather x1 -> x0, waiting for transfers between devices: 89.4 us -> none  [shards(): lax.all_gather(pixels, 'row', axis=2, tiled=True)]
    all_to_all x1 -> x4, blocking collectives: 16.9 us -> 67.5 us  [swap(): return lax.all_to_all(array, axes, 0, 0, tiled=True)]
    dot_general x2 -> x0, matrix products: 14.7 us -> none  [the longest x1 14.3 us: pair_rows(): jnp.einsum('vciw,vcjw->ij', own, others, precision=lax.Precision.HIGHEST,...]
    all_to_all x1, waiting for transfers between devices: 9.19 us -> 19.2 us  [swap(): return lax.all_to_all(array, axes, 0, 0, tiled=True)]
    pallas_call x0 -> x4, Pallas kernels: none -> 9.41 us  [the longest x1 3.59 us: shards(): call(pair_body, f32(4, 2, 256, LANES), (wide, wide), 1, 1)(place, rows)]
    unnamed x10 -> x0, local copies, waits for them, and re-layouts: 3.13 us -> none
    broadcast_in_dim x0 -> x2, local copies, waits for them, and re-layouts: none -> 2.17 us  [the longest x1 1.97 us: shards(): jnp.broadcast_to(own[None], (2, *own.shape)).reshape(16, *own.shape[1:])]
    all_to_all x2 -> x0, other arithmetic: 1.9 us -> none  [sum_at_owner(): parts = lax.all_to_all(split_up(array, dim, size), axis, 0, 0, tiled=True)]
  transfers between devices with their start and end apart: 2 -> 1, of which waited for: 2 -> 1; matrix products, arithmetic and copies ran while one was open for 0% -> 1% of each run, Pallas kernels for 0% -> 0%
where the time goes in v1:
time: 110 us; the launch traced here: 109 us
  blocking collectives  67.5 us (61%)
  waiting for transfers between devices  19.2 us (17%)
  starting transfers between devices  9.55 us (9%)
  Pallas kernels  9.41 us (9%)
  local copies, waits for them, and re-layouts  2.17 us (2%)
    all_to_all x4, blocking collectives, swap(): return lax.all_to_all(array, axes, 0, 0, tiled=True)  67.5 us
    all_to_all x1, waiting for transfers between devices, swap(): return lax.all_to_all(array, axes, 0, 0, tiled=True)  19.2 us
    all_to_all x1, starting transfers between devices, swap(): return lax.all_to_all(array, axes, 0, 0, tiled=True)  9.55 us
    pallas_call x1, Pallas kernels, shards(): call(pair_body, f32(4, 2, 256, LANES), (wide, wide), 1, 1)(place, rows)  3.59 us
  transfers between devices with their start and end apart: 1, of which 1 were waited for; matrix products, arithmetic and copies ran while one was open for 1% of the time, Pallas kernels for 0%

profile of v1, /device:TPU:1, one launch (start us, length us, event | category | flops | bytes accessed | tf_op | source)
XLA Modules:
  0.0 109.1 jit_solution(4616678839118501560)
XLA Ops:
  0.6 2.0 %broadcast_in_dim.14 = f32[2,8,96,128]{3,2,1,0:T(8,128)} broadcast(f32[8,96,128]{2,1,0:T(8,128)} %bitcast.11), dimensions={1,2,3} | broadcast | bytes 1179648 | tf_op jit(solution)/shard_map/broadcast_in_dim | solution.py:97
  2.6 9.6 %all-to-all-start = ((f32[16,96,128]{2,1,0:T(8,128)}), f32[16,96,128]{2,1,0:T(8,128)S(1)}, u32[]{:S(2)}, u32[]{:S(2)}) async-start(f32[16,96,128]{2,1,0:T(8,128)} %bitcast.3), calls=%async_computation | async-start | bytes 1572864 | tf_op jit(solution)/shard_map/all_to_all | solution.py:91
  12.2 0.6 pad_add_fusion.place
  12.8 19.2 %all-to-all-done = f32[16,96,128]{2,1,0:T(8,128)S(1)} async-done(((f32[16,96,128]{2,1,0:T(8,128)}), f32[16,96,128]{2,1,0:T(8,128)S(1)}, u32[]{:S(2)}, u32[]{:S(2)}) %all-to-all-start) | async-done | bytes 786464 | tf_op jit(solution)/shard_map/all_to_all | solution.py:91
  32.0 0.2 broadcast_in_dim.15
  32.2 7.8 %all_to_all.25.rows = f32[2,16,96,128]{3,2,1,0:T(8,128)} all-to-all(f32[2,16,96,128]{3,2,1,0:T(8,128)S(1)} %broadcast_in_dim.15), channel_id=1, replica_groups=mesh['zl'=2,'y'=8,'k'=2,'zh'=4,'x'=4] {'k'}, dimensions={0} | all-to-all | bytes 3145728 | tf_op jit(solution)/shard_map/all_to_all | solution.py:91
  40.0 3.6 %shard_map.41 = f32[4,2,256,128]{3,2,1,0:T(8,128)} custom-call(s32[2]{0:T(128)} %pad_add_fusion.place, f32[2,16,96,128]{3,2,1,0:T(8,128)} %all_to_all.25.rows), custom_call_target="tpu_custom_call" | custom-call | tf_op jit(solution)/shard_map/pallas_call | solution.py:100
  43.6 19.0 %all_to_all.26 = f32[4,512,128]{2,1,0:T(8,128)} all-to-all(f32[4,512,128]{2,1,0:T(8,128)} %bitcast.9), channel_id=1, replica_groups=mesh['zl'=2,'y'=8,'k'=2,'zh'=4,'x'=4] {'x'}, dimensions={0} | all-to-all | bytes 2097152 | tf_op jit(solution)/shard_map/all_to_all | solution.py:91
  62.6 2.1 %shard_map.42 = f32[4,8,16,128]{3,2,1,0:T(8,128)} custom-call(f32[4,2,256,128]{3,2,1,0:T(8,128)} %bitcast.8), custom_call_target="tpu_custom_call" | custom-call | tf_op jit(solution)/shard_map/pallas_call | solution.py:102
  64.6 23.8 %all_to_all.27.parts = f32[32,16,128]{2,1,0:T(8,128)} all-to-all(f32[32,16,128]{2,1,0:T(8,128)} %bitcast.10), channel_id=1, replica_groups=mesh['zl'=2,'y'=8,'k'=2,'zh'=4,'x'=4] {'zh','y'}, dimensions={0} | all-to-all | bytes 524288 | tf_op jit(solution)/shard_map/all_to_all | solution.py:91
  88.5 2.1 %shard_map.43 = (f32[32,64]{1,0:T(8,128)}, f32[32,8,128]{2,1,0:T(8,128)}) custom-call(f32[32,16,128]{2,1,0:T(8,128)} %all_to_all.27.parts, f32[32,512]{1,0:T(8,128)} %factor.1), custom_call_target="tpu_custom_call" | custom-call | tf_op jit(solution)/shard_map/pallas_call | solution.py:104
  90.6 16.9 %all_to_all.28.parts = f32[32,8,128]{2,1,0:T(8,128)} all-to-all(f32[32,8,128]{2,1,0:T(8,128)} %get-tuple-element.5), channel_id=1, replica_groups=mesh['zl'=2,'y'=8,'k'=2,'zh'=4,'x'=4] {'zl','y','k'}, dimensions={0} | all-to-all | bytes 262144 | tf_op jit(solution)/shard_map/all_to_all | solution.py:91
  107.5 1.6 %shard_map.44 = f32[16,64]{1,0:T(8,128)} custom-call(f32[32,8,128]{2,1,0:T(8,128)} %all_to_all.28.parts), custom_call_target="tpu_custom_call" | custom-call | tf_op jit(solution)/shard_map/pallas_call | solution.py:105
Async XLA Ops:
  2.6 29.4 %all-to-all-start = ((f32[16,96,128]{2,1,0:T(8,128)}), f32[16,96,128]{2,1,0:T(8,128)S(1)}, u32[]{:S(2)}, u32[]{:S(2)}) async-start(f32[16,96,128]{2,1,0:T(8,128)} %bitcast.3), calls=%async_computation | async-start | bytes 1572864 | tf_op jit(solution)/shard_map/all_to_all | solution.py:91

commit v2 on v1

--- a/solution.py
+++ b/solution.py
@@ -16,24 +16,28 @@
 NT = (((1,), (1,)), ((), ()))
 
 
-def call(body, out, scratch=(), operands=1, scalars=0):
+def call(body, out, scratch=(), operands=1):
     vmem = pl.BlockSpec(memory_space=pltpu.VMEM)
-    smem = pl.BlockSpec(memory_space=pltpu.SMEM)
     many = isinstance(out, tuple)
-    return pl.pallas_call(
+    kernel = pl.pallas_call(
         body,
         out_shape=out,
-        in_specs=[smem] * scalars + [vmem] * operands,
+        in_specs=[vmem] * operands,
         out_specs=tuple(vmem for _ in out) if many else vmem,
         scratch_shapes=list(scratch),
     )
+    return lambda *arrays: kernel(*(pltpu.with_memory_space_constraint(a, pltpu.VMEM) for a in arrays))
 
 
 def f32(*shape):
+    return pltpu.VMEM(shape, jnp.float32)
+
+
+def result(*shape):
     return jax.ShapeDtypeStruct(shape, jnp.float32)
 
 
-def pair_body(place, rows, out, high, low):
+def pair_body(rows, out, high, low):
     for x in range(4):
         for zl in range(2):
             for zh_lo in range(2):
@@ -44,7 +48,7 @@
                         h = v.astype(jnp.bfloat16)
                         high[at : at + OWN, p * LANES : (p + 1) * LANES] = h
                         low[at : at + OWN, p * LANES : (p + 1) * LANES] = (v - h.astype(jnp.float32)).astype(jnp.bfloat16)
-    own = place[0] * 128 + place[1] * 32
+    own = lax.axis_index("zl") * 128 + lax.axis_index("k") * 32
 
     def own_rows(ref):
         return jnp.concatenate([ref[pl.ds(pl.multiple_of(own + (y % 4) * 256 + (y // 4) * 64, 32), OWN), :] for y in range(8)], axis=0)
@@ -91,18 +95,21 @@
     return lax.all_to_all(array, axes, 0, 0, tiled=True)
 
 
+def both(array, axis):
+    return swap(jnp.broadcast_to(array[None], (2, *array.shape)), axis)
+
+
 def shards(pixels, factor):
-    place = jnp.stack([lax.axis_index("zl"), lax.axis_index("k")]).astype(jnp.int32)
     own = pixels.reshape(8, PLANES * OWN, LANES)
-    rows = swap(jnp.broadcast_to(own[None], (2, *own.shape)).reshape(16, *own.shape[1:]), ("zl", "y"))
-    rows = swap(jnp.broadcast_to(rows[None], (2, *rows.shape)), "k")
+    rows = both(swap(own, "y"), "zl")
+    rows = both(rows.reshape(16, *own.shape[1:]), "k")
     wide = pltpu.VMEM((1024, DEPTH), jnp.bfloat16)
-    partial_gram = call(pair_body, f32(4, 2, 256, LANES), (wide, wide), 1, 1)(place, rows)
+    partial_gram = call(pair_body, f32(4, 2, 256, LANES), (wide, wide))(rows)
     partial_gram = swap(partial_gram.reshape(4, 512, LANES), "x").reshape(4, 2, 256, LANES)
     folded = call(fold_body, f32(4, 8, 16, LANES))(partial_gram)
     folded = swap(folded.reshape(32, 16, LANES), ("zh", "y"))
-    gram, term = call(term_body, (f32(32, 64), f32(32, 8, LANES)), (), 2)(folded, factor)
-    projected = call(close_body, f32(16, 64))(swap(term, ROW))
+    gram, term = call(term_body, (result(32, 64), f32(32, 8, LANES)), (), 2)(folded, factor)
+    projected = call(close_body, result(16, 64))(swap(term, ROW))
     return gram, projected.T
 
 

time: 110 us -> 102 us (0.927)
  blocking collectives: 67.5 us -> 97.5 us
  waiting for transfers between devices: 19.2 us -> 0 us
  starting transfers between devices: 9.55 us -> 0 us
  Pallas kernels: 9.41 us -> 2.75 us
  local copies, waits for them, and re-layouts: 2.17 us -> 0.28 us
    all_to_all x4 -> x6, blocking collectives: 67.5 us -> 97.5 us  [swap(): return lax.all_to_all(array, axes, 0, 0, tiled=True)]
    all_to_all x1 -> x0, waiting for transfers between devices: 19.2 us -> none  [swap(): return lax.all_to_all(array, axes, 0, 0, tiled=True)]
    all_to_all x1 -> x0, starting transfers between devices: 9.55 us -> none  [swap(): return lax.all_to_all(array, axes, 0, 0, tiled=True)]
    pallas_call x4, Pallas kernels: 9.41 us -> 2.75 us  [call(): kernel(*(pltpu.with_memory_space_constraint(a, pltpu.VMEM) for a in arrays))]
    broadcast_in_dim x2, local copies, waits for them, and re-layouts: 2.17 us -> 0.27 us  [both(): return swap(jnp.broadcast_to(array[None], (2, *array.shape)), axis)]
  transfers between devices with their start and end apart: 1 -> 0, of which waited for: 1 -> 0; matrix products, arithmetic and copies ran while one was open for 1% -> 0% of each run, Pallas kernels for 0% -> 0%
where the time goes in v2:
time: 102 us; the launch traced here: 101 us
  blocking collectives  97.5 us (96%)
  Pallas kernels  2.75 us (3%)
    all_to_all x6, blocking collectives, swap(): return lax.all_to_all(array, axes, 0, 0, tiled=True)  97.5 us
    pallas_call x4, Pallas kernels, call(): kernel(*(pltpu.with_memory_space_constraint(a, pltpu.VMEM) for a in arrays))  2.75 us

profile of v2, /device:TPU:1, one launch (start us, length us, event | category | flops | bytes accessed | tf_op | source)
XLA Modules:
  0.0 101.2 jit_solution(14757120464462846234)
XLA Ops:
  0.6 19.2 %all_to_all.30 = f32[8,96,128]{2,1,0:T(8,128)S(1)} all-to-all(f32[8,96,128]{2,1,0:T(8,128)} %bitcast.10), channel_id=1, replica_groups=mesh['zl'=2,'y'=8,'k'=2,'zh'=4,'x'=4] {'y'}, dimensions={0} | all-to-all | bytes 786432 | tf_op jit(solution)/shard_map/all_to_all | solution.py:95
  19.8 0.1 broadcast_in_dim.6
  19.9 13.7 %all_to_all.31 = f32[2,8,96,128]{3,2,1,0:T(8,128)S(1)} all-to-all(f32[2,8,96,128]{3,2,1,0:T(8,128)S(1)} %broadcast_in_dim.6), channel_id=1, replica_groups=mesh['zl'=2,'y'=8,'k'=2,'zh'=4,'x'=4] {'zl'}, dimensions={0} | all-to-all | bytes 1572864 | tf_op jit(solution)/shard_map/all_to_all | solution.py:95
  33.6 0.2 broadcast_in_dim.15
  33.8 7.8 %all_to_all.32.rows = f32[2,16,96,128]{3,2,1,0:T(8,128)S(1)} all-to-all(f32[2,16,96,128]{3,2,1,0:T(8,128)S(1)} %broadcast_in_dim.15), channel_id=1, replica_groups=mesh['zl'=2,'y'=8,'k'=2,'zh'=4,'x'=4] {'k'}, dimensions={0} | all-to-all | bytes 3145728 | tf_op jit(solution)/shard_map/all_to_all | solution.py:95
  41.7 1.2 %shard_map.41 = f32[4,2,256,128]{3,2,1,0:T(8,128)S(1)} custom-call(f32[2,16,96,128]{3,2,1,0:T(8,128)S(1)} %all_to_all.32.rows), custom_call_target="tpu_custom_call" | custom-call | tf_op jit(solution)/shard_map/pallas_call | solution.py:29
  42.9 0.0 copy-start
  42.9 18.2 %all_to_all.33 = f32[4,512,128]{2,1,0:T(8,128)S(1)} all-to-all(f32[4,512,128]{2,1,0:T(8,128)S(1)} %bitcast.7), channel_id=1, replica_groups=mesh['zl'=2,'y'=8,'k'=2,'zh'=4,'x'=4] {'x'}, dimensions={0} | all-to-all | bytes 2097152 | tf_op jit(solution)/shard_map/all_to_all | solution.py:95
  61.1 0.1 shard_map.42
  61.2 22.7 %all_to_all.34.parts = f32[32,16,128]{2,1,0:T(8,128)S(1)} all-to-all(f32[32,16,128]{2,1,0:T(8,128)S(1)} %bitcast.8), channel_id=1, replica_groups=mesh['zl'=2,'y'=8,'k'=2,'zh'=4,'x'=4] {'zh','y'}, dimensions={0} | all-to-all | bytes 524288 | tf_op jit(solution)/shard_map/all_to_all | solution.py:95
  83.9 0.0 copy-done
  83.9 0.7 shard_map.43
  84.7 15.8 %all_to_all.35.parts = f32[32,8,128]{2,1,0:T(8,128)S(1)} all-to-all(f32[32,8,128]{2,1,0:T(8,128)S(1)} %get-tuple-element.5), channel_id=1, replica_groups=mesh['zl'=2,'y'=8,'k'=2,'zh'=4,'x'=4] {'zl','y','k'}, dimensions={0} | all-to-all | bytes 262144 | tf_op jit(solution)/shard_map/all_to_all | solution.py:95
  100.5 0.7 shard_map.44
Async XLA Ops:
  42.9 41.1 %copy-start = (f32[32,512]{1,0:T(8,128)S(1)}, f32[32,512]{1,0:T(8,128)}, u32[]{:S(2)}) copy-start(f32[32,512]{1,0:T(8,128)} %factor.1) | copy-start | bytes 196612

commit v3 on v2

--- a/solution.py
+++ b/solution.py
@@ -6,9 +6,9 @@
 from jax.sharding import Mesh
 from jax.sharding import PartitionSpec as P
 
-AXES = ("zl", "y", "k", "zh", "x")
-SIZES = (2, 8, 2, 4, 4)
-ROW = ("zl", "y", "k")
+AXES = ("zl", "yh", "yl", "k", "zh", "x")
+SIZES = (2, 4, 2, 2, 4, 4)
+ROW = ("zl", "yh", "yl", "k")
 COL = ("zh", "x")
 PLANES, OWN, LANES = 3, 32, 128
 DEPTH = PLANES * LANES
@@ -51,7 +51,8 @@
     own = lax.axis_index("zl") * 128 + lax.axis_index("k") * 32
 
     def own_rows(ref):
-        return jnp.concatenate([ref[pl.ds(pl.multiple_of(own + (y % 4) * 256 + (y // 4) * 64, 32), OWN), :] for y in range(8)], axis=0)
+        order = [yh * 2 + yl for yl in range(2) for yh in range(4)]
+        return jnp.concatenate([ref[pl.ds(pl.multiple_of(own + (y % 4) * 256 + (y // 4) * 64, 32), OWN), :] for y in order], axis=0)
 
     own_high, own_low = own_rows(high), own_rows(low)
     for x in range(4):
@@ -59,17 +60,18 @@
         g = lax.dot_general(own_high, l, NT, preferred_element_type=jnp.float32)
         g += lax.dot_general(own_low, h, NT, preferred_element_type=jnp.float32)
         g += lax.dot_general(own_high, h, NT, preferred_element_type=jnp.float32)
-        out[x, 0] = g[:, :LANES]
-        out[x, 1] = g[:, LANES:]
+        for yl in range(2):
+            for zl in range(2):
+                out[x, yl, zl] = g[yl * 128 : (yl + 1) * 128, zl * LANES : (zl + 1) * LANES]
 
 
 def fold_body(parts, out):
     left = lax.broadcasted_iota(jnp.int32, (16, LANES), 1) < 64
     for zh in range(2):
-        for y in range(8):
+        for y in range(4):
             v = parts[0, zh, y * OWN : (y + 1) * OWN, :]
-            for x in range(1, 4):
-                v += parts[x, zh, y * OWN : (y + 1) * OWN, :]
+            for src in range(1, 8):
+                v += parts[src, zh, y * OWN : (y + 1) * OWN, :]
             a, b = v[:16], v[16:]
             out[zh * 2, y] = jnp.where(left, a, pltpu.roll(b, 64, 1))
             out[zh * 2 + 1, y] = jnp.where(left, pltpu.roll(a, 64, 1), b)
@@ -101,13 +103,13 @@
 
 def shards(pixels, factor):
     own = pixels.reshape(8, PLANES * OWN, LANES)
-    rows = both(swap(own, "y"), "zl")
-    rows = both(rows.reshape(16, *own.shape[1:]), "k")
+    rows = swap(jnp.concatenate([own, own]), ("zl", "yh", "yl"))
+    rows = both(rows, "k")
     wide = pltpu.VMEM((1024, DEPTH), jnp.bfloat16)
-    partial_gram = call(pair_body, f32(4, 2, 256, LANES), (wide, wide))(rows)
-    partial_gram = swap(partial_gram.reshape(4, 512, LANES), "x").reshape(4, 2, 256, LANES)
-    folded = call(fold_body, f32(4, 8, 16, LANES))(partial_gram)
-    folded = swap(folded.reshape(32, 16, LANES), ("zh", "y"))
+    partial_gram = call(pair_body, f32(4, 2, 2, 128, LANES), (wide, wide))(rows)
+    partial_gram = swap(partial_gram.reshape(8, 256, LANES), ("x", "yl"))
+    folded = call(fold_body, f32(4, 4, 16, LANES))(partial_gram.reshape(8, 2, 128, LANES))
+    folded = swap(folded.reshape(16, 16, LANES), ("zh", "yh"))
     gram, term = call(term_body, (result(32, 64), f32(32, 8, LANES)), (), 2)(folded, factor)
     projected = call(close_body, result(16, 64))(swap(term, ROW))
     return gram, projected.T

time: 102 us -> 98.9 us (0.970)
  blocking collectives: 97.5 us -> 93.8 us
  other arithmetic: 0 us -> 1.17 us
    all_to_all x6 -> x5, blocking collectives: 97.5 us -> 93.8 us  [swap(): return lax.all_to_all(array, axes, 0, 0, tiled=True)]
    concatenate x0 -> x1, other arithmetic: none -> 1.17 us  [shards(): rows = swap(jnp.concatenate([own, own]), ('zl', 'yh', 'yl'))]
where the time goes in v3:
time: 98.9 us; the launch traced here: 98.6 us
  blocking collectives  93.8 us (95%)
  Pallas kernels  2.72 us (3%)
  other arithmetic  1.17 us (1%)
    all_to_all x5, blocking collectives, swap(): return lax.all_to_all(array, axes, 0, 0, tiled=True)  93.8 us
    pallas_call x4, Pallas kernels, call(): kernel(*(pltpu.with_memory_space_constraint(a, pltpu.VMEM) for a in arrays))  2.72 us

profile of v3, /device:TPU:1, one launch (start us, length us, event | category | flops | bytes accessed | tf_op | source)
XLA Modules:
  0.0 98.6 jit_solution(17688636693407799955)
XLA Ops:
  0.6 1.2 %pad_maximum_fusion = f32[16,96,128]{2,1,0:T(8,128)S(1)} fusion(f32[8,96,128]{2,1,0:T(8,128)} %bitcast.8), kind=kLoop, calls=%fused_computation | loop fusion | flops 196608 | bytes 1179648 | tf_op jit(solution)/shard_map/concatenate | solution.py:106
  1.8 29.5 %all_to_all.25 = f32[16,96,128]{2,1,0:T(8,128)S(1)} all-to-all(f32[16,96,128]{2,1,0:T(8,128)S(1)} %pad_maximum_fusion), channel_id=1, replica_groups=mesh['zl'=2,'yh'=4,'yl'=2,'k'=2,'zh'=4,'x'=4] {'zl','yh','yl'}, dimensions={0} | all-to-all | bytes 1572864 | tf_op jit(solution)/shard_map/all_to_all | solution.py:97
  31.3 0.2 broadcast_in_dim.2
  31.5 6.8 %all_to_all.26.rows = f32[2,16,96,128]{3,2,1,0:T(8,128)S(1)} all-to-all(f32[2,16,96,128]{3,2,1,0:T(8,128)S(1)} %broadcast_in_dim.2), channel_id=1, replica_groups=mesh['zl'=2,'yh'=4,'yl'=2,'k'=2,'zh'=4,'x'=4] {'k'}, dimensions={0} | all-to-all | bytes 3145728 | tf_op jit(solution)/shard_map/all_to_all | solution.py:97
  38.4 1.2 %shard_map.41 = f32[4,2,2,128,128]{4,3,2,1,0:T(8,128)S(1)} custom-call(f32[2,16,96,128]{3,2,1,0:T(8,128)S(1)} %all_to_all.26.rows), custom_call_target="tpu_custom_call" | custom-call | tf_op jit(solution)/shard_map/pallas_call | solution.py:29
  39.6 0.0 copy-start
  39.6 20.3 %all_to_all.27 = f32[8,256,128]{2,1,0:T(8,128)S(1)} all-to-all(f32[8,256,128]{2,1,0:T(8,128)S(1)} %bitcast.5), channel_id=1, replica_groups=mesh['zl'=2,'yh'=4,'yl'=2,'k'=2,'zh'=4,'x'=4] {'x','yl'}, dimensions={0} | all-to-all | bytes 2097152 | tf_op jit(solution)/shard_map/all_to_all | solution.py:97
  59.9 0.1 shard_map.42
  60.0 22.2 %all_to_all.28.parts = f32[16,16,128]{2,1,0:T(8,128)S(1)} all-to-all(f32[16,16,128]{2,1,0:T(8,128)S(1)} %bitcast.7), channel_id=1, replica_groups=mesh['zl'=2,'yh'=4,'yl'=2,'k'=2,'zh'=4,'x'=4] {'zh','yh'}, dimensions={0} | all-to-all | bytes 262144 | tf_op jit(solution)/shard_map/all_to_all | solution.py:97
  82.2 0.0 copy-done
  82.2 0.7 shard_map.43
  82.9 14.9 %all_to_all.29.parts = f32[32,8,128]{2,1,0:T(8,128)S(1)} all-to-all(f32[32,8,128]{2,1,0:T(8,128)S(1)} %get-tuple-element.5), channel_id=1, replica_groups=mesh['zl'=2,'yh'=4,'yl'=2,'k'=2,'zh'=4,'x'=4] {'zl','yh','yl','k'}, dimensions={0} | all-to-all | bytes 262144 | tf_op jit(solution)/shard_map/all_to_all | solution.py:97
  97.9 0.7 shard_map.44
Async XLA Ops:
  39.6 42.7 %copy-start = (f32[32,512]{1,0:T(8,128)S(1)}, f32[32,512]{1,0:T(8,128)}, u32[]{:S(2)}) copy-start(f32[32,512]{1,0:T(8,128)} %factor.1) | copy-start | bytes 196612

commit v4 on v3

--- a/solution.py
+++ b/solution.py
@@ -6,9 +6,9 @@
 from jax.sharding import Mesh
 from jax.sharding import PartitionSpec as P
 
-AXES = ("zl", "yh", "yl", "k", "zh", "x")
-SIZES = (2, 4, 2, 2, 4, 4)
-ROW = ("zl", "yh", "yl", "k")
+AXES = ("zl", "yo", "ya", "yb", "k", "zh", "x")
+SIZES = (2, 2, 2, 2, 2, 4, 4)
+ROW = ("zl", "yo", "ya", "yb", "k")
 COL = ("zh", "x")
 PLANES, OWN, LANES = 3, 32, 128
 DEPTH = PLANES * LANES
@@ -48,11 +48,11 @@
                         h = v.astype(jnp.bfloat16)
                         high[at : at + OWN, p * LANES : (p + 1) * LANES] = h
                         low[at : at + OWN, p * LANES : (p + 1) * LANES] = (v - h.astype(jnp.float32)).astype(jnp.bfloat16)
-    own = lax.axis_index("zl") * 128 + lax.axis_index("k") * 32
+    own = lax.axis_index("yo") * 64 + lax.axis_index("k") * 32
 
     def own_rows(ref):
-        order = [yh * 2 + yl for yl in range(2) for yh in range(4)]
-        return jnp.concatenate([ref[pl.ds(pl.multiple_of(own + (y % 4) * 256 + (y // 4) * 64, 32), OWN), :] for y in order], axis=0)
+        order = [(ya * 2 + yb) * 256 + zl * 128 for yb in range(2) for zl in range(2) for ya in range(2)]
+        return jnp.concatenate([ref[pl.ds(pl.multiple_of(own + at, 32), OWN), :] for at in order], axis=0)
 
     own_high, own_low = own_rows(high), own_rows(low)
     for x in range(4):
@@ -60,21 +60,23 @@
         g = lax.dot_general(own_high, l, NT, preferred_element_type=jnp.float32)
         g += lax.dot_general(own_low, h, NT, preferred_element_type=jnp.float32)
         g += lax.dot_general(own_high, h, NT, preferred_element_type=jnp.float32)
-        for yl in range(2):
-            for zl in range(2):
-                out[x, yl, zl] = g[yl * 128 : (yl + 1) * 128, zl * LANES : (zl + 1) * LANES]
+        for yb in range(2):
+            for zh in range(2):
+                out[x, yb, zh] = g[yb * 128 : (yb + 1) * 128, zh * LANES : (zh + 1) * LANES]
 
 
 def fold_body(parts, out):
     left = lax.broadcasted_iota(jnp.int32, (16, LANES), 1) < 64
     for zh in range(2):
-        for y in range(4):
-            v = parts[0, zh, y * OWN : (y + 1) * OWN, :]
-            for src in range(1, 8):
-                v += parts[src, zh, y * OWN : (y + 1) * OWN, :]
-            a, b = v[:16], v[16:]
-            out[zh * 2, y] = jnp.where(left, a, pltpu.roll(b, 64, 1))
-            out[zh * 2 + 1, y] = jnp.where(left, pltpu.roll(a, 64, 1), b)
+        for zl in range(2):
+            for ya in range(2):
+                at = (zl * 2 + ya) * OWN
+                v = parts[0, zh, at : at + OWN, :]
+                for src in range(1, 8):
+                    v += parts[src, zh, at : at + OWN, :]
+                a, b = v[:16], v[16:]
+                out[zl, zh * 2, ya] = jnp.where(left, a, pltpu.roll(b, 64, 1))
+                out[zl, zh * 2 + 1, ya] = jnp.where(left, pltpu.roll(a, 64, 1), b)
 
 
 def term_body(parts, factor, gram, term):
@@ -102,14 +104,14 @@
 
 
 def shards(pixels, factor):
-    own = pixels.reshape(8, PLANES * OWN, LANES)
-    rows = swap(jnp.concatenate([own, own]), ("zl", "yh", "yl"))
+    own = pixels.reshape(2, 1, 4, PLANES * OWN, LANES)
+    rows = swap(jnp.concatenate([own, own], axis=1).reshape(16, PLANES * OWN, LANES), ("zl", "yo", "ya", "yb"))
     rows = both(rows, "k")
     wide = pltpu.VMEM((1024, DEPTH), jnp.bfloat16)
     partial_gram = call(pair_body, f32(4, 2, 2, 128, LANES), (wide, wide))(rows)
-    partial_gram = swap(partial_gram.reshape(8, 256, LANES), ("x", "yl"))
-    folded = call(fold_body, f32(4, 4, 16, LANES))(partial_gram.reshape(8, 2, 128, LANES))
-    folded = swap(folded.reshape(16, 16, LANES), ("zh", "yh"))
+    partial_gram = swap(partial_gram.reshape(8, 256, LANES), ("x", "yb"))
+    folded = call(fold_body, f32(2, 4, 2, 16, LANES))(partial_gram.reshape(8, 2, 128, LANES))
+    folded = swap(folded.reshape(16, 16, LANES), ("zl", "zh", "ya"))
     gram, term = call(term_body, (result(32, 64), f32(32, 8, LANES)), (), 2)(folded, factor)
     projected = call(close_body, result(16, 64))(swap(term, ROW))
     return gram, projected.T

time: 98.9 us -> 97.7 us (0.988)
  blocking collectives: 93.8 us -> 92.6 us
    all_to_all x5, blocking collectives: 93.8 us -> 92.6 us  [swap(): return lax.all_to_all(array, axes, 0, 0, tiled=True)]
where the time goes in v4:
time: 97.7 us; the launch traced here: 97.4 us
  blocking collectives  92.6 us (95%)
  Pallas kernels  2.67 us (3%)
  other arithmetic  1.17 us (1%)
    all_to_all x5, blocking collectives, swap(): return lax.all_to_all(array, axes, 0, 0, tiled=True)  92.6 us
    pallas_call x4, Pallas kernels, call(): kernel(*(pltpu.with_memory_space_constraint(a, pltpu.VMEM) for a in arrays))  2.67 us

profile of v4, /device:TPU:1, one launch (start us, length us, event | category | flops | bytes accessed | tf_op | source)
XLA Modules:
  0.0 97.4 jit_solution(5002763034230132344)
XLA Ops:
  0.6 1.2 %pad_maximum_fusion = f32[2,2,4,96,128]{4,3,2,0,1:T(8,128)S(1)} fusion(f32[2,1,4,96,128]{4,3,2,0,1:T(8,128)} %bitcast.10), kind=kLoop, calls=%fused_computation | loop fusion | flops 196608 | bytes 1179648 | tf_op jit(solution)/shard_map/concatenate | solution.py:108
  1.8 0.1 copy.4
  1.9 29.5 %all_to_all.25 = f32[16,96,128]{2,1,0:T(8,128)S(1)} all-to-all(f32[16,96,128]{2,1,0:T(8,128)S(1)} %bitcast.9), channel_id=1, replica_groups=mesh['zl'=2,'yo'=2,'ya'=2,'yb'=2,'k'=2,'zh'=4,'x'=4] {'zl','yo','ya','yb'}, dimensions={0} | all-to-all | bytes 1572864 | tf_op jit(solution)/shard_map/all_to_all | solution.py:99
  31.4 0.2 broadcast_in_dim.2
  31.6 6.8 %all_to_all.26.rows = f32[2,16,96,128]{3,2,1,0:T(8,128)S(1)} all-to-all(f32[2,16,96,128]{3,2,1,0:T(8,128)S(1)} %broadcast_in_dim.2), channel_id=1, replica_groups=mesh['zl'=2,'yo'=2,'ya'=2,'yb'=2,'k'=2,'zh'=4,'x'=4] {'k'}, dimensions={0} | all-to-all | bytes 3145728 | tf_op jit(solution)/shard_map/all_to_all | solution.py:99
  38.4 1.2 %shard_map.41 = f32[4,2,2,128,128]{4,3,2,1,0:T(8,128)S(1)} custom-call(f32[2,16,96,128]{3,2,1,0:T(8,128)S(1)} %all_to_all.26.rows), custom_call_target="tpu_custom_call" | custom-call | tf_op jit(solution)/shard_map/pallas_call | solution.py:29
  39.6 0.0 copy-start
  39.6 20.3 %all_to_all.27 = f32[8,256,128]{2,1,0:T(8,128)S(1)} all-to-all(f32[8,256,128]{2,1,0:T(8,128)S(1)} %bitcast.6), channel_id=1, replica_groups=mesh['zl'=2,'yo'=2,'ya'=2,'yb'=2,'k'=2,'zh'=4,'x'=4] {'x','yb'}, dimensions={0} | all-to-all | bytes 2097152 | tf_op jit(solution)/shard_map/all_to_all | solution.py:99
  59.9 0.1 shard_map.42
  60.0 18.4 %all_to_all.28.parts = f32[16,16,128]{2,1,0:T(8,128)S(1)} all-to-all(f32[16,16,128]{2,1,0:T(8,128)S(1)} %bitcast.8), channel_id=1, replica_groups=mesh['zl'=2,'yo'=2,'ya'=2,'yb'=2,'k'=2,'zh'=4,'x'=4] {'zl','zh','ya'}, dimensions={0} | all-to-all | bytes 262144 | tf_op jit(solution)/shard_map/all_to_all | solution.py:99
  78.4 0.0 copy-done
  78.4 0.7 shard_map.43
  79.1 17.6 %all_to_all.29.parts = f32[32,8,128]{2,1,0:T(8,128)S(1)} all-to-all(f32[32,8,128]{2,1,0:T(8,128)S(1)} %get-tuple-element.5), channel_id=1, replica_groups=mesh['zl'=2,'yo'=2,'ya'=2,'yb'=2,'k'=2,'zh'=4,'x'=4] {'zl','yo','ya','yb..., dimensions={0} | all-to-all | bytes 262144 | tf_op jit(solution)/shard_map/all_to_all | solution.py:99
  96.7 0.7 shard_map.44
Async XLA Ops:
  39.6 38.8 %copy-start = (f32[32,512]{1,0:T(8,128)S(1)}, f32[32,512]{1,0:T(8,128)}, u32[]{:S(2)}) copy-start(f32[32,512]{1,0:T(8,128)} %factor.1) | copy-start | bytes 196612

commit v5 on v4

--- a/solution.py
+++ b/solution.py
@@ -44,7 +44,7 @@
                 for k in range(2):
                     at = x * 256 + zl * 128 + zh_lo * 64 + k * 32
                     for p in range(PLANES):
-                        v = rows[k, zl * 8 + zh_lo * 4 + x, p * OWN : (p + 1) * OWN, :]
+                        v = rows[k, zh_lo * 8 + zl * 4 + x, p * OWN : (p + 1) * OWN, :]
                         h = v.astype(jnp.bfloat16)
                         high[at : at + OWN, p * LANES : (p + 1) * LANES] = h
                         low[at : at + OWN, p * LANES : (p + 1) * LANES] = (v - h.astype(jnp.float32)).astype(jnp.bfloat16)
@@ -60,23 +60,21 @@
         g = lax.dot_general(own_high, l, NT, preferred_element_type=jnp.float32)
         g += lax.dot_general(own_low, h, NT, preferred_element_type=jnp.float32)
         g += lax.dot_general(own_high, h, NT, preferred_element_type=jnp.float32)
-        for yb in range(2):
+        for at in range(4):
             for zh in range(2):
-                out[x, yb, zh] = g[yb * 128 : (yb + 1) * 128, zh * LANES : (zh + 1) * LANES]
+                out[x, at, zh] = g[at * 64 : (at + 1) * 64, zh * LANES : (zh + 1) * LANES]
 
 
 def fold_body(parts, out):
     left = lax.broadcasted_iota(jnp.int32, (16, LANES), 1) < 64
     for zh in range(2):
-        for zl in range(2):
-            for ya in range(2):
-                at = (zl * 2 + ya) * OWN
-                v = parts[0, zh, at : at + OWN, :]
-                for src in range(1, 8):
-                    v += parts[src, zh, at : at + OWN, :]
-                a, b = v[:16], v[16:]
-                out[zl, zh * 2, ya] = jnp.where(left, a, pltpu.roll(b, 64, 1))
-                out[zl, zh * 2 + 1, ya] = jnp.where(left, pltpu.roll(a, 64, 1), b)
+        for y in range(2):
+            v = parts[0, zh, y * OWN : (y + 1) * OWN, :]
+            for src in range(1, 16):
+                v += parts[src, zh, y * OWN : (y + 1) * OWN, :]
+            a, b = v[:16], v[16:]
+            out[zh * 2, y] = jnp.where(left, a, pltpu.roll(b, 64, 1))
+            out[zh * 2 + 1, y] = jnp.where(left, pltpu.roll(a, 64, 1), b)
 
 
 def term_body(parts, factor, gram, term):
@@ -90,7 +88,8 @@
         term[r] = jnp.concatenate([t[r * 16 : r * 16 + 8], t[r * 16 + 8 : r * 16 + 16]], axis=1)
 
 
-def close_body(parts, out):
+def close_body(parts, block, gram, out):
+    gram[...] = block[...]
     v = jnp.sum(parts[...], axis=0)
     out[...] = jnp.concatenate([v[:, :64], v[:, 64:]], axis=0)
 
@@ -104,16 +103,16 @@
 
 
 def shards(pixels, factor):
-    own = pixels.reshape(2, 1, 4, PLANES * OWN, LANES)
-    rows = swap(jnp.concatenate([own, own], axis=1).reshape(16, PLANES * OWN, LANES), ("zl", "yo", "ya", "yb"))
+    own = pixels.reshape(8, PLANES * OWN, LANES)
+    rows = swap(jnp.concatenate([own, own]), ("yo", "zl", "ya", "yb"))
     rows = both(rows, "k")
     wide = pltpu.VMEM((1024, DEPTH), jnp.bfloat16)
-    partial_gram = call(pair_body, f32(4, 2, 2, 128, LANES), (wide, wide))(rows)
-    partial_gram = swap(partial_gram.reshape(8, 256, LANES), ("x", "yb"))
-    folded = call(fold_body, f32(2, 4, 2, 16, LANES))(partial_gram.reshape(8, 2, 128, LANES))
-    folded = swap(folded.reshape(16, 16, LANES), ("zl", "zh", "ya"))
-    gram, term = call(term_body, (result(32, 64), f32(32, 8, LANES)), (), 2)(folded, factor)
-    projected = call(close_body, result(16, 64))(swap(term, ROW))
+    partial_gram = call(pair_body, f32(4, 4, 2, 64, LANES), (wide, wide))(rows)
+    partial_gram = swap(partial_gram.reshape(16, 128, LANES), ("x", "yb", "zl"))
+    folded = call(fold_body, f32(4, 2, 16, LANES))(partial_gram.reshape(16, 2, 64, LANES))
+    folded = swap(folded.reshape(8, 16, LANES), ("zh", "ya"))
+    block, term = call(term_body, (f32(32, 64), f32(32, 8, LANES)), (), 2)(folded, factor)
+    gram, projected = call(close_body, (result(32, 64), result(16, 64)), (), 2)(swap(term, ROW), block)
     return gram, projected.T
 
 

time: 97.7 us -> 97.3 us (level)
  no operation moved by 1% of the time
where the time goes in v5:
time: 97.3 us; the launch traced here: 96.9 us
  blocking collectives  92.4 us (95%)
  Pallas kernels  2.49 us (3%)
  other arithmetic  1.17 us (1%)
    all_to_all x5, blocking collectives, swap(): return lax.all_to_all(array, axes, 0, 0, tiled=True)  92.4 us
    pallas_call x4, Pallas kernels, call(): kernel(*(pltpu.with_memory_space_constraint(a, pltpu.VMEM) for a in arrays))  2.49 us

profile of v5, /device:TPU:1, one launch (start us, length us, event | category | flops | bytes accessed | tf_op | source)
XLA Modules:
  0.0 96.9 jit_solution(3426359275970775726)
XLA Ops:
  0.6 1.2 %pad_maximum_fusion = f32[16,96,128]{2,1,0:T(8,128)S(1)} fusion(f32[8,96,128]{2,1,0:T(8,128)} %bitcast.8), kind=kLoop, calls=%fused_computation | loop fusion | flops 196608 | bytes 1179648 | tf_op jit(solution)/shard_map/concatenate | solution.py:107
  1.8 29.6 %all_to_all.25 = f32[16,96,128]{2,1,0:T(8,128)S(1)} all-to-all(f32[16,96,128]{2,1,0:T(8,128)S(1)} %pad_maximum_fusion), channel_id=1, replica_groups=mesh['zl'=2,'yo'=2,'ya'=2,'yb'=2,'k'=2,'zh'=4,'x'=4] {'yo','zl','ya','yb'}, dimensions={0} | all-to-all | bytes 1572864 | tf_op jit(solution)/shard_map/all_to_all | solution.py:98
  31.4 0.2 broadcast_in_dim.2
  31.6 6.9 %all_to_all.26.rows = f32[2,16,96,128]{3,2,1,0:T(8,128)S(1)} all-to-all(f32[2,16,96,128]{3,2,1,0:T(8,128)S(1)} %broadcast_in_dim.2), channel_id=1, replica_groups=mesh['zl'=2,'yo'=2,'ya'=2,'yb'=2,'k'=2,'zh'=4,'x'=4] {'k'}, dimensions={0} | all-to-all | bytes 3145728 | tf_op jit(solution)/shard_map/all_to_all | solution.py:98
  38.5 1.2 %shard_map.41 = f32[4,4,2,64,128]{4,3,2,1,0:T(8,128)S(1)} custom-call(f32[2,16,96,128]{3,2,1,0:T(8,128)S(1)} %all_to_all.26.rows), custom_call_target="tpu_custom_call" | custom-call | tf_op jit(solution)/shard_map/pallas_call | solution.py:29
  39.7 0.0 copy-start
  39.7 21.3 %all_to_all.27 = f32[16,128,128]{2,1,0:T(8,128)S(1)} all-to-all(f32[16,128,128]{2,1,0:T(8,128)S(1)} %bitcast.5), channel_id=1, replica_groups=mesh['zl'=2,'yo'=2,'ya'=2,'yb'=2,'k'=2,'zh'=4,'x'=4] {'x','yb','zl'}, dimensions={0} | all-to-all | bytes 2097152 | tf_op jit(solution)/shard_map/all_to_all | solution.py:98
  61.0 0.1 shard_map.42
  61.1 17.6 %all_to_all.28.parts = f32[8,16,128]{2,1,0:T(8,128)S(1)} all-to-all(f32[8,16,128]{2,1,0:T(8,128)S(1)} %bitcast.7), channel_id=1, replica_groups=mesh['zl'=2,'yo'=2,'ya'=2,'yb'=2,'k'=2,'zh'=4,'x'=4] {'zh','ya'}, dimensions={0} | all-to-all | bytes 131072 | tf_op jit(solution)/shard_map/all_to_all | solution.py:98
  78.8 0.0 copy-done
  78.8 0.5 shard_map.43
  79.3 17.0 %all_to_all.29.parts = f32[32,8,128]{2,1,0:T(8,128)S(1)} all-to-all(f32[32,8,128]{2,1,0:T(8,128)S(1)} %get-tuple-element.6), channel_id=1, replica_groups=mesh['zl'=2,'yo'=2,'ya'=2,'yb'=2,'k'=2,'zh'=4,'x'=4] {'zl','yo','ya','yb..., dimensions={0} | all-to-all | bytes 262144 | tf_op jit(solution)/shard_map/all_to_all | solution.py:98
  96.2 0.7 shard_map.44
Async XLA Ops:
  39.7 39.1 %copy-start = (f32[32,512]{1,0:T(8,128)S(1)}, f32[32,512]{1,0:T(8,128)}, u32[]{:S(2)}) copy-start(f32[32,512]{1,0:T(8,128)} %factor.1) | copy-start | bytes 196612

commit v6 on v5

--- a/solution.py
+++ b/solution.py
@@ -37,18 +37,19 @@
     return jax.ShapeDtypeStruct(shape, jnp.float32)
 
 
-def pair_body(rows, out, high, low):
+def pair_body(mine, theirs, out, high, low):
+    core = lax.axis_index("k")
     for x in range(4):
         for zl in range(2):
             for zh_lo in range(2):
-                for k in range(2):
-                    at = x * 256 + zl * 128 + zh_lo * 64 + k * 32
+                for rows, k in ((mine, core), (theirs, 1 - core)):
+                    at = pl.multiple_of(x * 256 + zl * 128 + zh_lo * 64 + k * 32, 32)
                     for p in range(PLANES):
-                        v = rows[k, zh_lo * 8 + zl * 4 + x, p * OWN : (p + 1) * OWN, :]
+                        v = rows[zh_lo * 8 + zl * 4 + x, p * OWN : (p + 1) * OWN, :]
                         h = v.astype(jnp.bfloat16)
-                        high[at : at + OWN, p * LANES : (p + 1) * LANES] = h
-                        low[at : at + OWN, p * LANES : (p + 1) * LANES] = (v - h.astype(jnp.float32)).astype(jnp.bfloat16)
-    own = lax.axis_index("yo") * 64 + lax.axis_index("k") * 32
+                        high[pl.ds(at, OWN), p * LANES : (p + 1) * LANES] = h
+                        low[pl.ds(at, OWN), p * LANES : (p + 1) * LANES] = (v - h.astype(jnp.float32)).astype(jnp.bfloat16)
+    own = lax.axis_index("yo") * 64 + core * 32
 
     def own_rows(ref):
         order = [(ya * 2 + yb) * 256 + zl * 128 for yb in range(2) for zl in range(2) for ya in range(2)]
@@ -98,16 +99,12 @@
     return lax.all_to_all(array, axes, 0, 0, tiled=True)
 
 
-def both(array, axis):
-    return swap(jnp.broadcast_to(array[None], (2, *array.shape)), axis)
-
-
 def shards(pixels, factor):
     own = pixels.reshape(8, PLANES * OWN, LANES)
     rows = swap(jnp.concatenate([own, own]), ("yo", "zl", "ya", "yb"))
-    rows = both(rows, "k")
+    theirs = lax.ppermute(rows, "k", [(0, 1), (1, 0)])
     wide = pltpu.VMEM((1024, DEPTH), jnp.bfloat16)
-    partial_gram = call(pair_body, f32(4, 4, 2, 64, LANES), (wide, wide))(rows)
+    partial_gram = call(pair_body, f32(4, 4, 2, 64, LANES), (wide, wide), 2)(rows, theirs)
     partial_gram = swap(partial_gram.reshape(16, 128, LANES), ("x", "yb", "zl"))
     folded = call(fold_body, f32(4, 2, 16, LANES))(partial_gram.reshape(16, 2, 64, LANES))
     folded = swap(folded.reshape(8, 16, LANES), ("zh", "ya"))

time: 97.3 us -> 96.3 us (0.990)
  blocking collectives: 92.4 us -> 85.5 us
  starting transfers between devices: 0 us -> 4.19 us
  waiting for transfers between devices: 0 us -> 1.89 us
    all_to_all x5 -> x4, blocking collectives: 92.4 us -> 85.5 us  [swap(): return lax.all_to_all(array, axes, 0, 0, tiled=True)]
    ppermute x0 -> x1, starting transfers between devices: none -> 4.19 us  [shards(): theirs = lax.ppermute(rows, 'k', [(0, 1), (1, 0)])]
    ppermute x0 -> x1, waiting for transfers between devices: none -> 1.89 us  [shards(): theirs = lax.ppermute(rows, 'k', [(0, 1), (1, 0)])]
  transfers between devices with their start and end apart: 0 -> 1, of which waited for: 0 -> 1; matrix products, arithmetic and copies ran while one was open for 0% -> 0% of each run, Pallas kernels for 0% -> 0%
where the time goes in v6:
time: 96.3 us; the launch traced here: 96 us
  blocking collectives  85.5 us (89%)
  starting transfers between devices  4.19 us (4%)
  Pallas kernels  2.6 us (3%)
  waiting for transfers between devices  1.89 us (2%)
  other arithmetic  1.17 us (1%)
    all_to_all x4, blocking collectives, swap(): return lax.all_to_all(array, axes, 0, 0, tiled=True)  85.5 us
    ppermute x1, starting transfers between devices, shards(): theirs = lax.ppermute(rows, 'k', [(0, 1), (1, 0)])  4.19 us
    pallas_call x4, Pallas kernels, call(): kernel(*(pltpu.with_memory_space_constraint(a, pltpu.VMEM) for a in arrays))  2.6 us
  transfers between devices with their start and end apart: 1, of which 1 were waited for; matrix products, arithmetic and copies ran while one was open for 0% of the time, Pallas kernels for 0%

profile of v6, /device:TPU:1, one launch (start us, length us, event | category | flops | bytes accessed | tf_op | source)
XLA Modules:
  0.0 96.0 jit_solution(6566359705384260812)
XLA Ops:
  0.6 1.2 %pad_maximum_fusion = f32[16,96,128]{2,1,0:T(8,128)S(1)} fusion(f32[8,96,128]{2,1,0:T(8,128)} %bitcast.8), kind=kLoop, calls=%fused_computation | loop fusion | flops 196608 | bytes 1179648 | tf_op jit(solution)/shard_map/concatenate | solution.py:104
  1.8 29.6 %all_to_all.20.mine = f32[16,96,128]{2,1,0:T(8,128)S(1)} all-to-all(f32[16,96,128]{2,1,0:T(8,128)S(1)} %pad_maximum_fusion), channel_id=1, replica_groups=mesh['zl'=2,'yo'=2,'ya'=2,'yb'=2,'k'=2,'zh'=4,'x'=4] {'yo','zl','ya','yb'}, dimensions={0} | all-to-all | bytes 1572864 | tf_op jit(solution)/shard_map/all_to_all | solution.py:99
  31.4 4.2 %collective-permute-start = (f32[16,96,128]{2,1,0:T(8,128)S(1)}, f32[16,96,128]{2,1,0:T(8,128)S(1)}, u32[]{:S(2)}, u32[]{:S(2)}) collective-permute-start(f32[16,96,128]{2,1,0:T(8,128)S(1)} %all_to_all.20.mine), channel_id=1, source_target_pairs={{0,16},{16,0},{1,17},{17,1},{2,18},{18,2},{3,19},{19,3},{4,20},{20... | collective-permute-start | bytes 2359304 | tf_op jit(solution)/shard_map/ppermute | solution.py:105
  35.6 1.9 %collective-permute-done.theirs = f32[16,96,128]{2,1,0:T(8,128)S(1)} collective-permute-done((f32[16,96,128]{2,1,0:T(8,128)S(1)}, f32[16,96,128]{2,1,0:T(8,128)S(1)}, u32[]{:S(2)}, u32[]{:S(2)}) %collective-permute-start) | collective-permute-done | bytes 786464 | tf_op jit(solution)/shard_map/ppermute | solution.py:105
  37.5 1.3 %shard_map.41 = f32[4,4,2,64,128]{4,3,2,1,0:T(8,128)S(1)} custom-call(f32[16,96,128]{2,1,0:T(8,128)S(1)} %all_to_all.20.mine, f32[16,96,128]{2,1,0:T(8,128)S(1)} %collective-permute-done.theirs), custom_call_target="tpu_custom_call" | custom-call | tf_op jit(solution)/shard_map/pallas_call | solution.py:29
  38.8 21.1 %all_to_all.21 = f32[16,128,128]{2,1,0:T(8,128)S(1)} all-to-all(f32[16,128,128]{2,1,0:T(8,128)S(1)} %bitcast.5), channel_id=1, replica_groups=mesh['zl'=2,'yo'=2,'ya'=2,'yb'=2,'k'=2,'zh'=4,'x'=4] {'x','yb','zl'}, dimensions={0} | all-to-all | bytes 2097152 | tf_op jit(solution)/shard_map/all_to_all | solution.py:99
  59.9 0.1 shard_map.42
  60.0 0.0 copy-start
  60.0 17.8 %all_to_all.22.parts = f32[8,16,128]{2,1,0:T(8,128)S(1)} all-to-all(f32[8,16,128]{2,1,0:T(8,128)S(1)} %bitcast.7), channel_id=1, replica_groups=mesh['zl'=2,'yo'=2,'ya'=2,'yb'=2,'k'=2,'zh'=4,'x'=4] {'zh','ya'}, dimensions={0} | all-to-all | bytes 131072 | tf_op jit(solution)/shard_map/all_to_all | solution.py:99
  77.8 0.0 copy-done
  77.8 0.5 shard_map.43
  78.3 17.0 %all_to_all.23.parts = f32[32,8,128]{2,1,0:T(8,128)S(1)} all-to-all(f32[32,8,128]{2,1,0:T(8,128)S(1)} %get-tuple-element.6), channel_id=1, replica_groups=mesh['zl'=2,'yo'=2,'ya'=2,'yb'=2,'k'=2,'zh'=4,'x'=4] {'zl','yo','ya','yb..., dimensions={0} | all-to-all | bytes 262144 | tf_op jit(solution)/shard_map/all_to_all | solution.py:99
  95.3 0.7 shard_map.44
Async XLA Ops:
  31.4 6.1 %collective-permute-start = (f32[16,96,128]{2,1,0:T(8,128)S(1)}, f32[16,96,128]{2,1,0:T(8,128)S(1)}, u32[]{:S(2)}, u32[]{:S(2)}) collective-permute-start(f32[16,96,128]{2,1,0:T(8,128)S(1)} %all_to_all.20.mine), channel_id=1, source_target_pairs={{0,16},{16,0},{1,17},{17,1},{2,18},{18,2},{3,19},{19,3},{4,20},{20... | collective-permute-start | bytes 2359304 | tf_op jit(solution)/shard_map/ppermute | solution.py:105
  60.0 17.8 %copy-start = (f32[32,512]{1,0:T(8,128)S(1)}, f32[32,512]{1,0:T(8,128)}, u32[]{:S(2)}) copy-start(f32[32,512]{1,0:T(8,128)} %factor.1) | copy-start | bytes 196612

commit v7 on v6

--- a/solution.py
+++ b/solution.py
@@ -35,6 +35,25 @@
 
 def result(*shape):
     return jax.ShapeDtypeStruct(shape, jnp.float32)
+
+
+def twice_body(pixels, out, done):
+    copies = [pltpu.make_async_copy(pixels.at[pl.ds(2 * i, 2)], out.at[pl.ds(2 * i, 2)], done.at[i]) for i in range(4)]
+    for copy in copies:
+        copy.start()
+    for i, copy in enumerate(copies):
+        copy.wait()
+        out[8 + 2 * i : 10 + 2 * i] = out[2 * i : 2 * i + 2]
+
+
+def twice(pixels):
+    return pl.pallas_call(
+        twice_body,
+        out_shape=pltpu.VMEM((16, *pixels.shape[1:]), jnp.float32),
+        in_specs=[pl.BlockSpec(memory_space=pltpu.HBM)],
+        out_specs=pl.BlockSpec(memory_space=pltpu.VMEM),
+        scratch_shapes=[pltpu.SemaphoreType.DMA((4,))],
+    )(pixels)
 
 
 def pair_body(mine, theirs, out, high, low):
@@ -101,7 +120,7 @@
 
 def shards(pixels, factor):
     own = pixels.reshape(8, PLANES * OWN, LANES)
-    rows = swap(jnp.concatenate([own, own]), ("yo", "zl", "ya", "yb"))
+    rows = swap(twice(own), ("yo", "zl", "ya", "yb"))
     theirs = lax.ppermute(rows, "k", [(0, 1), (1, 0)])
     wide = pltpu.VMEM((1024, DEPTH), jnp.bfloat16)
     partial_gram = call(pair_body, f32(4, 4, 2, 64, LANES), (wide, wide), 2)(rows, theirs)

time: 96.3 us -> 96.3 us (level)
  other arithmetic: 1.17 us -> 0 us
  Pallas kernels: 2.6 us -> 3.68 us
    concatenate x1 -> x0, other arithmetic: 1.17 us -> none  [shards(): rows = swap(jnp.concatenate([own, own]), ('yo', 'zl', 'ya', 'yb'))]
    pallas_call x0 -> x1, Pallas kernels: none -> 1.08 us  [twice(): pl.pallas_call(twice_body, out_shape=pltpu.VMEM((16, *pixels.shape[1:]),...]
where the time goes in v7:
time: 96.3 us; the launch traced here: 95.9 us
  blocking collectives  85.5 us (89%)
  starting transfers between devices  4.19 us (4%)
  Pallas kernels  3.68 us (4%)
  waiting for transfers between devices  1.89 us (2%)
    all_to_all x4, blocking collectives, swap(): return lax.all_to_all(array, axes, 0, 0, tiled=True)  85.5 us
    ppermute x1, starting transfers between devices, shards(): theirs = lax.ppermute(rows, 'k', [(0, 1), (1, 0)])  4.19 us
    pallas_call x4, Pallas kernels, call(): kernel(*(pltpu.with_memory_space_constraint(a, pltpu.VMEM) for a in arrays))  2.6 us
  transfers between devices with their start and end apart: 1, of which 1 were waited for; matrix products, arithmetic and copies ran while one was open for 0% of the time, Pallas kernels for 0%

profile of v7, /device:TPU:1, one launch (start us, length us, event | category | flops | bytes accessed | tf_op | source)
XLA Modules:
  0.0 95.9 jit_solution(16127593626496817042)
XLA Ops:
  0.6 1.1 %shard_map.41 = f32[16,96,128]{2,1,0:T(8,128)S(1)} custom-call(f32[8,96,128]{2,1,0:T(8,128)} %bitcast.8), custom_call_target="tpu_custom_call" | custom-call | tf_op jit(solution)/shard_map/pallas_call | solution.py:50
  1.7 29.6 %all_to_all.20.mine = f32[16,96,128]{2,1,0:T(8,128)S(1)} all-to-all(f32[16,96,128]{2,1,0:T(8,128)S(1)} %shard_map.41), channel_id=1, replica_groups=mesh['zl'=2,'yo'=2,'ya'=2,'yb'=2,'k'=2,'zh'=4,'x'=4] {'yo','zl','ya','yb'}, dimensions={0} | all-to-all | bytes 1572864 | tf_op jit(solution)/shard_map/all_to_all | solution.py:118
  31.3 4.2 %collective-permute-start = (f32[16,96,128]{2,1,0:T(8,128)S(1)}, f32[16,96,128]{2,1,0:T(8,128)S(1)}, u32[]{:S(2)}, u32[]{:S(2)}) collective-permute-start(f32[16,96,128]{2,1,0:T(8,128)S(1)} %all_to_all.20.mine), channel_id=1, source_target_pairs={{0,16},{16,0},{1,17},{17,1},{2,18},{18,2},{3,19},{19,3},{4,20},{20... | collective-permute-start | bytes 2359304 | tf_op jit(solution)/shard_map/ppermute | solution.py:124
  35.5 1.9 %collective-permute-done.theirs = f32[16,96,128]{2,1,0:T(8,128)S(1)} collective-permute-done((f32[16,96,128]{2,1,0:T(8,128)S(1)}, f32[16,96,128]{2,1,0:T(8,128)S(1)}, u32[]{:S(2)}, u32[]{:S(2)}) %collective-permute-start) | collective-permute-done | bytes 786464 | tf_op jit(solution)/shard_map/ppermute | solution.py:124
  37.4 1.3 %shard_map.42 = f32[4,4,2,64,128]{4,3,2,1,0:T(8,128)S(1)} custom-call(f32[16,96,128]{2,1,0:T(8,128)S(1)} %all_to_all.20.mine, f32[16,96,128]{2,1,0:T(8,128)S(1)} %collective-permute-done.theirs), custom_call_target="tpu_custom_call" | custom-call | tf_op jit(solution)/shard_map/pallas_call | solution.py:29
  38.7 21.1 %all_to_all.21 = f32[16,128,128]{2,1,0:T(8,128)S(1)} all-to-all(f32[16,128,128]{2,1,0:T(8,128)S(1)} %bitcast.5), channel_id=1, replica_groups=mesh['zl'=2,'yo'=2,'ya'=2,'yb'=2,'k'=2,'zh'=4,'x'=4] {'x','yb','zl'}, dimensions={0} | all-to-all | bytes 2097152 | tf_op jit(solution)/shard_map/all_to_all | solution.py:118
  59.8 0.1 shard_map.43
  59.9 0.0 copy-start
  60.0 17.8 %all_to_all.22.parts = f32[8,16,128]{2,1,0:T(8,128)S(1)} all-to-all(f32[8,16,128]{2,1,0:T(8,128)S(1)} %bitcast.7), channel_id=1, replica_groups=mesh['zl'=2,'yo'=2,'ya'=2,'yb'=2,'k'=2,'zh'=4,'x'=4] {'zh','ya'}, dimensions={0} | all-to-all | bytes 131072 | tf_op jit(solution)/shard_map/all_to_all | solution.py:118
  77.7 0.0 copy-done
  77.7 0.5 shard_map.44
  78.2 17.0 %all_to_all.23.parts = f32[32,8,128]{2,1,0:T(8,128)S(1)} all-to-all(f32[32,8,128]{2,1,0:T(8,128)S(1)} %get-tuple-element.6), channel_id=1, replica_groups=mesh['zl'=2,'yo'=2,'ya'=2,'yb'=2,'k'=2,'zh'=4,'x'=4] {'zl','yo','ya','yb..., dimensions={0} | all-to-all | bytes 262144 | tf_op jit(solution)/shard_map/all_to_all | solution.py:118
  95.2 0.7 shard_map.45
Async XLA Ops:
  31.3 6.1 %collective-permute-start = (f32[16,96,128]{2,1,0:T(8,128)S(1)}, f32[16,96,128]{2,1,0:T(8,128)S(1)}, u32[]{:S(2)}, u32[]{:S(2)}) collective-permute-start(f32[16,96,128]{2,1,0:T(8,128)S(1)} %all_to_all.20.mine), channel_id=1, source_target_pairs={{0,16},{16,0},{1,17},{17,1},{2,18},{18,2},{3,19},{19,3},{4,20},{20... | collective-permute-start | bytes 2359304 | tf_op jit(solution)/shard_map/ppermute | solution.py:124
  59.9 17.8 %copy-start = (f32[32,512]{1,0:T(8,128)S(1)}, f32[32,512]{1,0:T(8,128)}, u32[]{:S(2)}) copy-start(f32[32,512]{1,0:T(8,128)} %factor.1) | copy-start | bytes 196612

commit v8 on v6

--- a/solution.py
+++ b/solution.py
@@ -37,18 +37,29 @@
     return jax.ShapeDtypeStruct(shape, jnp.float32)
 
 
-def pair_body(mine, theirs, out, high, low):
-    core = lax.axis_index("k")
+def split_rows(rows, high, low, first, stride):
     for x in range(4):
         for zl in range(2):
             for zh_lo in range(2):
-                for rows, k in ((mine, core), (theirs, 1 - core)):
-                    at = pl.multiple_of(x * 256 + zl * 128 + zh_lo * 64 + k * 32, 32)
-                    for p in range(PLANES):
-                        v = rows[zh_lo * 8 + zl * 4 + x, p * OWN : (p + 1) * OWN, :]
-                        h = v.astype(jnp.bfloat16)
-                        high[pl.ds(at, OWN), p * LANES : (p + 1) * LANES] = h
-                        low[pl.ds(at, OWN), p * LANES : (p + 1) * LANES] = (v - h.astype(jnp.float32)).astype(jnp.bfloat16)
+                at = pl.multiple_of(first + (x * 4 + zl * 2 + zh_lo) * stride, 32)
+                for p in range(PLANES):
+                    v = rows[zh_lo * 8 + zl * 4 + x, p * OWN : (p + 1) * OWN, :]
+                    h = v.astype(jnp.bfloat16)
+                    high[pl.ds(at, OWN), p * LANES : (p + 1) * LANES] = h
+                    low[pl.ds(at, OWN), p * LANES : (p + 1) * LANES] = (v - h.astype(jnp.float32)).astype(jnp.bfloat16)
+
+
+def mine_body(mine, both):
+    split_rows(mine, both.at[0], both.at[1], 0, 32)
+
+
+def pair_body(theirs, mine, out, high, low):
+    core = lax.axis_index("k")
+    for block in range(16):
+        at = pl.multiple_of(block * 64 + core * 32, 32)
+        high[pl.ds(at, OWN), :] = mine[0, block * OWN : (block + 1) * OWN, :]
+        low[pl.ds(at, OWN), :] = mine[1, block * OWN : (block + 1) * OWN, :]
+    split_rows(theirs, high, low, (1 - core) * 32, 64)
     own = lax.axis_index("yo") * 64 + core * 32
 
     def own_rows(ref):
@@ -104,7 +115,8 @@
     rows = swap(jnp.concatenate([own, own]), ("yo", "zl", "ya", "yb"))
     theirs = lax.ppermute(rows, "k", [(0, 1), (1, 0)])
     wide = pltpu.VMEM((1024, DEPTH), jnp.bfloat16)
-    partial_gram = call(pair_body, f32(4, 4, 2, 64, LANES), (wide, wide), 2)(rows, theirs)
+    mine = call(mine_body, pltpu.VMEM((2, 512, DEPTH), jnp.bfloat16))(rows)
+    partial_gram = call(pair_body, f32(4, 4, 2, 64, LANES), (wide, wide), 2)(theirs, mine)
     partial_gram = swap(partial_gram.reshape(16, 128, LANES), ("x", "yb", "zl"))
     folded = call(fold_body, f32(4, 2, 16, LANES))(partial_gram.reshape(16, 2, 64, LANES))
     folded = swap(folded.reshape(8, 16, LANES), ("zh", "ya"))

time: 96.3 us -> 96.3 us (level)
    pallas_call x4 -> x5, Pallas kernels: 2.6 us -> 2.7 us  [call(): kernel(*(pltpu.with_memory_space_constraint(a, pltpu.VMEM) for a in arrays))]
where the time goes in v8:
time: 96.3 us; the launch traced here: 96 us
  blocking collectives  85.5 us (89%)
  starting transfers between devices  4.19 us (4%)
  Pallas kernels  2.7 us (3%)
  waiting for transfers between devices  1.75 us (2%)
  other arithmetic  1.17 us (1%)
    all_to_all x4, blocking collectives, swap(): return lax.all_to_all(array, axes, 0, 0, tiled=True)  85.5 us
    ppermute x1, starting transfers between devices, shards(): theirs = lax.ppermute(rows, 'k', [(0, 1), (1, 0)])  4.19 us
    pallas_call x5, Pallas kernels, call(): kernel(*(pltpu.with_memory_space_constraint(a, pltpu.VMEM) for a in arrays))  2.7 us
  transfers between devices with their start and end apart: 1, of which 1 were waited for; matrix products, arithmetic and copies ran while one was open for 0% of the time, Pallas kernels for 0%

profile of v8, /device:TPU:1, one launch (start us, length us, event | category | flops | bytes accessed | tf_op | source)
XLA Modules:
  0.0 96.0 jit_solution(17425021537231232270)
XLA Ops:
  0.6 1.2 %pad_maximum_fusion = f32[16,96,128]{2,1,0:T(8,128)S(1)} fusion(f32[8,96,128]{2,1,0:T(8,128)} %bitcast.8), kind=kLoop, calls=%fused_computation | loop fusion | flops 196608 | bytes 1179648 | tf_op jit(solution)/shard_map/concatenate | solution.py:115
  1.8 29.6 %all_to_all.20.mine = f32[16,96,128]{2,1,0:T(8,128)S(1)} all-to-all(f32[16,96,128]{2,1,0:T(8,128)S(1)} %pad_maximum_fusion), channel_id=1, replica_groups=mesh['zl'=2,'yo'=2,'ya'=2,'yb'=2,'k'=2,'zh'=4,'x'=4] {'yo','zl','ya','yb'}, dimensions={0} | all-to-all | bytes 1572864 | tf_op jit(solution)/shard_map/all_to_all | solution.py:110
  31.4 4.2 %collective-permute-start = (f32[16,96,128]{2,1,0:T(8,128)S(1)}, f32[16,96,128]{2,1,0:T(8,128)S(1)}, u32[]{:S(2)}, u32[]{:S(2)}) collective-permute-start(f32[16,96,128]{2,1,0:T(8,128)S(1)} %all_to_all.20.mine), channel_id=1, source_target_pairs={{0,16},{16,0},{1,17},{17,1},{2,18},{18,2},{3,19},{19,3},{4,20},{20... | collective-permute-start | bytes 2359304 | tf_op jit(solution)/shard_map/ppermute | solution.py:116
  35.6 0.1 shard_map.41.mine
  35.7 1.8 %collective-permute-done.theirs = f32[16,96,128]{2,1,0:T(8,128)S(1)} collective-permute-done((f32[16,96,128]{2,1,0:T(8,128)S(1)}, f32[16,96,128]{2,1,0:T(8,128)S(1)}, u32[]{:S(2)}, u32[]{:S(2)}) %collective-permute-start) | collective-permute-done | bytes 786464 | tf_op jit(solution)/shard_map/ppermute | solution.py:116
  37.5 1.2 %shard_map.42 = f32[4,4,2,64,128]{4,3,2,1,0:T(8,128)S(1)} custom-call(f32[16,96,128]{2,1,0:T(8,128)S(1)} %collective-permute-done.theirs, bf16[2,512,384]{2,1,0:T(8,128)(2,1)S(1)} %shard_map.41.mine), custom_call_target="tpu_custom_call" | custom-call | tf_op jit(solution)/shard_map/pallas_call | solution.py:29
  38.7 21.1 %all_to_all.21 = f32[16,128,128]{2,1,0:T(8,128)S(1)} all-to-all(f32[16,128,128]{2,1,0:T(8,128)S(1)} %bitcast.5), channel_id=1, replica_groups=mesh['zl'=2,'yo'=2,'ya'=2,'yb'=2,'k'=2,'zh'=4,'x'=4] {'x','yb','zl'}, dimensions={0} | all-to-all | bytes 2097152 | tf_op jit(solution)/shard_map/all_to_all | solution.py:110
  59.9 0.1 shard_map.43
  60.0 0.0 copy-start
  60.0 17.8 %all_to_all.22.parts = f32[8,16,128]{2,1,0:T(8,128)S(1)} all-to-all(f32[8,16,128]{2,1,0:T(8,128)S(1)} %bitcast.7), channel_id=1, replica_groups=mesh['zl'=2,'yo'=2,'ya'=2,'yb'=2,'k'=2,'zh'=4,'x'=4] {'zh','ya'}, dimensions={0} | all-to-all | bytes 131072 | tf_op jit(solution)/shard_map/all_to_all | solution.py:110
  77.8 0.0 copy-done
  77.8 0.5 shard_map.44
  78.3 17.0 %all_to_all.23.parts = f32[32,8,128]{2,1,0:T(8,128)S(1)} all-to-all(f32[32,8,128]{2,1,0:T(8,128)S(1)} %get-tuple-element.6), channel_id=1, replica_groups=mesh['zl'=2,'yo'=2,'ya'=2,'yb'=2,'k'=2,'zh'=4,'x'=4] {'zl','yo','ya','yb..., dimensions={0} | all-to-all | bytes 262144 | tf_op jit(solution)/shard_map/all_to_all | solution.py:110
  95.3 0.7 shard_map.45
Async XLA Ops:
  31.4 6.1 %collective-permute-start = (f32[16,96,128]{2,1,0:T(8,128)S(1)}, f32[16,96,128]{2,1,0:T(8,128)S(1)}, u32[]{:S(2)}, u32[]{:S(2)}) collective-permute-start(f32[16,96,128]{2,1,0:T(8,128)S(1)} %all_to_all.20.mine), channel_id=1, source_target_pairs={{0,16},{16,0},{1,17},{17,1},{2,18},{18,2},{3,19},{19,3},{4,20},{20... | collective-permute-start | bytes 2359304 | tf_op jit(solution)/shard_map/ppermute | solution.py:116
  60.0 17.8 %copy-start = (f32[32,512]{1,0:T(8,128)S(1)}, f32[32,512]{1,0:T(8,128)}, u32[]{:S(2)}) copy-start(f32[32,512]{1,0:T(8,128)} %factor.1) | copy-start | bytes 196612
